TPU v7x, 32 devices: a whole 2x2x4 slice. The times are simulated.
32 devices in a mesh: rows: 32 (over z, y, x, core).
Axes of the slice: x: 2, y: 2, z: 4, core: 2. Of those that a mesh axis runs over, the one named last changes fastest.
Arguments:
- adj_diag: int32 [512, 512], P('rows'), may hold values from -2147483648 to 2147483647
- adj_right: int32 [512, 512], P('rows'), may hold values from -2147483648 to 2147483647
- alive_diag: int32 [512, 512], P('rows'), may hold values from -2147483648 to 2147483647
- alive_right: int32 [512, 512], P('rows'), may hold values from -2147483648 to 2147483647
- truss_k: int32 [1], replicated, may hold values from 130 to 193
Outputs:
- support_field: float32 [16384, 1024], P('rows')
- removed_counts: int32 [3], replicated
All inputs are finite; a program needn't handle non-finite values.
Results may differ from a plain program's by a relative error of at most 0.0003.
Values may be sent and summed in bfloat16 or wider, within the bound.
A program may use at most 64 MiB of HBM per device.

v0:
```python
import jax
import jax.numpy as jnp
from jax import lax
from jax.sharding import PartitionSpec as P

ITERS = 3


def shifted(array, axis, by):
    count = lax.axis_size(axis)
    return lax.ppermute(array, axis, [(i, (i + by) % count) for i in range(count)])


def unpack_tile(packed):
    shifts = jnp.arange(32, dtype=jnp.int32)
    tile_bits = packed[:, None, :] >> shifts[None, :, None] & 1
    return tile_bits.reshape(packed.shape[0] * 32, packed.shape[1])


def pack_bits(tile_bits):
    shifts = jnp.arange(32, dtype=jnp.int32)
    sectioned = tile_bits.reshape(tile_bits.shape[0] // 32, 32, tile_bits.shape[1])
    return jnp.sum(sectioned << shifts[None, :, None], axis=1, dtype=jnp.int32)


def within_tile(packed):
    upper_half = jnp.triu(unpack_tile(packed), 1)
    return (upper_half + upper_half.T).astype(jnp.bfloat16)


def across_tile(packed):
    return unpack_tile(packed).astype(jnp.bfloat16)


def pack_across(across):
    return pack_bits(across.astype(jnp.int32))


def fold_within(within):
    width = within.shape[0]
    half = width // 2
    row_ids = lax.broadcasted_iota(jnp.int32, (half, width), 0)
    col_ids = lax.broadcasted_iota(jnp.int32, (half, width), 1)
    flipped = within[half:][::-1, ::-1]
    folded = jnp.where(col_ids > row_ids, within[:half], flipped)
    return pack_bits(folded.astype(jnp.int32))


def unfold_within(packed):
    folded = unpack_tile(packed)
    half = folded.shape[0]
    width = folded.shape[1]
    row_ids = lax.broadcasted_iota(jnp.int32, (half, width), 0)
    col_ids = lax.broadcasted_iota(jnp.int32, (half, width), 1)
    top_rows = jnp.where(col_ids > row_ids, folded, jnp.zeros_like(folded))
    bottom_rows = jnp.where(col_ids < row_ids, folded, jnp.zeros_like(folded))[::-1, ::-1]
    upper_half = jnp.concatenate([top_rows, bottom_rows], axis=0)
    return (upper_half + upper_half.T).astype(jnp.bfloat16)


def support_within(prev_across, within, across):
    inside = lax.dot_general(
        prev_across, prev_across, (((0,), (0,)), ((), ())), preferred_element_type=jnp.float32
    )
    inside = inside + jnp.dot(within, within, preferred_element_type=jnp.float32)
    return inside + lax.dot_general(
        across, across, (((1,), (1,)), ((), ())), preferred_element_type=jnp.float32
    )


def support_across(within, across, next_within):
    between = jnp.dot(within, across, preferred_element_type=jnp.float32)
    return between + jnp.dot(across, next_within, preferred_element_type=jnp.float32)


def keep_edges(support, tile_mask, thresh):
    return jnp.where(support >= thresh, tile_mask, jnp.zeros_like(tile_mask))


def peel(prev_across, within, across, next_within, thresh):
    inside = support_within(prev_across, within, across)
    between = support_across(within, across, next_within)
    return (
        inside,
        between,
        keep_edges(inside, within, thresh),
        keep_edges(between, across, thresh),
    )


def tally(within, new_within, across, new_across):
    removed = jnp.sum((within - new_within).astype(jnp.int32)) // 2
    removed = removed + jnp.sum((across - new_across).astype(jnp.int32))
    return removed


def on_device(adj_diag, adj_right, alive_diag, alive_right, truss_k):
    within = within_tile(adj_diag & alive_diag)
    across_words = adj_right & alive_right
    across = across_tile(across_words)
    thresh = (truss_k[0] - 2).astype(jnp.float32)
    counts = []
    for step in range(ITERS):
        prev_across = across_tile(shifted(pack_across(across), "rows", 1))
        next_within = unfold_within(shifted(fold_within(within), "rows", -1))
        inside, between, new_within, new_across = peel(
            prev_across, within, across, next_within, thresh
        )
        counts.append(tally(within, new_within, across, new_across))
        within, across = (new_within, new_across)
    stacked = jnp.stack(counts)
    stacked = lax.psum(stacked, "rows")
    support = jnp.concatenate(
        [inside * within.astype(jnp.float32), between * across.astype(jnp.float32)], axis=1
    )
    return (support, stacked)


def solution(mesh):
    in_specs = (P("rows", None), P("rows", None), P("rows", None), P("rows", None), P())
    out_specs = (P("rows", None), P())
    return jax.shard_map(
        on_device, mesh=mesh, in_specs=in_specs, out_specs=out_specs, check_vma=False
    )
```

profile of v0, /device:TPU:0, one launch (start us, length us, event | category | flops | bytes accessed | tf_op | source)
XLA Modules:
  0.0 112.1 jit_solution(5490259086250720770)
XLA Ops:
  0.7 0.1 shift_right_arithmetic.162
  0.7 0.8 and.74
  1.5 0.2 fusion.17
  1.7 0.3 copy.7
  2.1 0.3 fusion.14
  2.4 0.9 rev.18
  3.4 0.1 fusion.25
  3.5 6.5 %collective-permute-start.1 = (s32[8,512]{1,0:T(8,128)S(1)}, s32[8,512]{1,0:T(8,128)S(1)}, u32[]{:S(2)}, u32[]{:S(2)}) collective-permute-start(s32[8,512]{1,0:T(8,128)S(1)} %fusion.25), channel_id=1, source_target_pairs={{0,31},{1,0},{2,1},{3,2},{4,3},{5,4},{6,5},{7,6},{8,7},{9,8},{10,9... | collective-permute-start | bytes 49160 | tf_op jit(solution)/shard_map/ppermute | solution.py:11
  9.9 0.4 and_convert_fusion.3
  10.4 1.4 %fusion.47 = f32[512,512]{1,0:T(8,128)} fusion(bf16[512,512]{1,0:T(8,128)(2,1)S(1)} %get-tuple-element.17, bf16[512,512]{1,0:T(8,128)(2,1)S(1)} %get-tuple-element.16), kind=kOutput, calls=%fused_computation.93 | convolution fusion | flops 268435456 | bytes 2097152 | tf_op jit(solution)/shard_map/dot_general | solution.py:72
  11.8 0.1 shift_left.64
  12.6 0.1 fusion.34
  12.7 0.8 rev.19
  13.5 1.1 pad_add_fusion
  14.5 2.6 %copy.8 = s32[512,512]{0,1:T(8,128)} copy(s32[512,512]{1,0:T(8,128)} %pad_add_fusion) | data formatting | bytes 2097152 | tf_op jit(solution)/shard_map/concatenate | solution.py:57
  17.1 2.2 %fusion.8 = (s32[16,512]{1,0:T(8,128)S(1)}, bf16[512,512]{1,0:T(8,128)(2,1)S(1)}) fusion(bf16[512,512]{1,0:T(8,128)(2,1)S(1)} %get-tuple-element.16, f32[]{:T(128)} %bitcast.4, f32[512,512]{1,0:T(8,128)} %fusion.47, s32[512,512]{0,1:T(8,128)} %copy.8, s32[256,512]{1,0:T(8,128)S(1)} %rev.19, s32[256,512]{1,0:T(8,128)S(1)} %get-tuple-element.14), kind=kOutput, calls=%fused_computation.25 | convolution fusion | flops 270786560 | bytes 4227076 | tf_op jit(solution)/shard_map/dot_general | solution.py:73
  19.4 0.5 convolution_bitcast_fusion.2
  19.9 0.4 convolution_add_fusion.8
  20.4 0.5 fusion.7
  20.9 0.9 rev.20
  21.8 0.1 fusion.24
  22.0 5.4 %collective-permute-start.2 = (s32[8,512]{1,0:T(8,128)S(1)}, s32[8,512]{1,0:T(8,128)S(1)}, u32[]{:S(2)}, u32[]{:S(2)}) collective-permute-start(s32[8,512]{1,0:T(8,128)S(1)} %fusion.24), channel_id=1, source_target_pairs={{0,31},{1,0},{2,1},{3,2},{4,3},{5,4},{6,5},{7,6},{8,7},{9,8},{10,9... | collective-permute-start | bytes 49160 | tf_op jit(solution)/shard_map/ppermute | solution.py:11
  27.3 0.5 convolution_bitcast_fusion
  27.8 0.4 convolution_add_fusion.4
  28.2 0.5 fusion.6
  28.8 0.9 rev.22
  29.7 0.1 fusion.23
  29.8 0.5 collective-permute-start.5
  30.4 1.4 %fusion.48 = f32[512,512]{1,0:T(8,128)} fusion(bf16[512,512]{1,0:T(8,128)(2,1)S(1)} %fusion.7, bf16[512,512]{1,0:T(8,128)(2,1)S(1)} %get-tuple-element.21), kind=kOutput, calls=%fused_computation.94 | convolution fusion | flops 268435456 | bytes 2097152 | tf_op jit(solution)/shard_map/dot_general | solution.py:72
  31.8 1.4 %fusion.28 = (s32[256,512]{1,0:T(8,128)}, s32[256,512]{1,0:T(8,128)}, s32[256,512]{1,0:T(8,128)}, s32[256,512]{1,0:T(8,128)S(1)}) fusion(s32[8,512]{1,0:T(8,128)S(1)} %collective-permute-done.5, s32[256]{0:T(256)S(1)} %shift_left.64, s32[8,512]{1,0:T(8,128)S(1)} %collective-permute-done.2), kind=kLoop, calls=%fused_computation.69 | loop fusion | flops 1310720 | bytes 2130944 | tf_op jit(solution)/shard_map/jit(_where)/select_n | solution.py:55
  33.2 3.9 %rev.21 = s32[256,512]{1,0:T(8,128)S(1)} reverse(s32[256,512]{1,0:T(8,128)} %get-tuple-element.18), dimensions={0,1} | reverse | bytes 1048576 | tf_op jit(solution)/shard_map/rev | solution.py:56
  37.1 1.1 pad_add_fusion.1
  38.2 2.6 %copy.9 = s32[512,512]{0,1:T(8,128)} copy(s32[512,512]{1,0:T(8,128)} %pad_add_fusion.1) | data formatting | bytes 2097152 | tf_op jit(solution)/shard_map/concatenate | solution.py:57
  40.7 2.4 %fusion.9 = (s32[16,512]{1,0:T(8,128)S(1)}, bf16[512,512]{1,0:T(8,128)(2,1)S(1)}) fusion(bf16[512,512]{1,0:T(8,128)(2,1)S(1)} %get-tuple-element.21, f32[]{:T(128)} %bitcast.4, f32[512,512]{1,0:T(8,128)} %fusion.48, s32[512,512]{0,1:T(8,128)} %copy.9, s32[256,512]{1,0:T(8,128)S(1)} %rev.21, s32[256,512]{1,0:T(8,128)} %copy-done.1), kind=kOutput, calls=%fused_computation.27 | convolution fusion | flops 270786560 | bytes 4227076 | tf_op jit(solution)/shard_map/dot_general | solution.py:73
  43.2 3.8 %rev.23 = s32[256,512]{1,0:T(8,128)S(1)} reverse(s32[256,512]{1,0:T(8,128)} %get-tuple-element.11), dimensions={0,1} | reverse | bytes 1048576 | tf_op jit(solution)/shard_map/rev | solution.py:56
  47.0 2.1 %pad_add_fusion.2 = s32[512,512]{1,0:T(8,128)} fusion(s32[256,512]{1,0:T(8,128)S(1)} %rev.23, s32[256,512]{1,0:T(8,128)} %get-tuple-element.10), kind=kLoop, calls=%fused_computation.23 | loop fusion | flops 262144 | bytes 2097152 | tf_op jit(solution)/shard_map/concatenate | solution.py:57
  49.1 2.5 %copy.13 = s32[512,512]{0,1:T(8,128)} copy(s32[512,512]{1,0:T(8,128)} %pad_add_fusion.2) | data formatting | bytes 2097152 | tf_op jit(solution)/shard_map/concatenate | solution.py:57
  51.7 0.4 fusion.49
  52.1 0.6 copy-done
  52.7 0.3 copy-done.3
  53.0 1.5 %convert_multiply_fusion = (f32[512,512]{1,0:T(8,128)}, f32[512,512]{1,0:T(8,128)S(1)}) fusion(bf16[512,512]{1,0:T(8,128)(2,1)S(1)} %get-tuple-element.25, f32[]{:T(128)} %bitcast.4, f32[512,512]{1,0:T(8,128)S(1)} %fusion.49, s32[512,512]{0,1:T(8,128)S(1)} %copy-done.3, s32[256,512]{1,0:T(8,128)S(1)} %rev.23, s32[256,512]{1,0:T(8,128)S(1)} %copy-done), kind=kOutput, calls=%fused_computation.48 | convolution fusion | flops 270532608 | bytes 5767172 | tf_op jit(solution)/shard_map/dot_general | solution.py:73
  54.5 1.5 %convert_reduce_fusion.4 = (s32[]{:T(128)}, s32[]{:T(128)}, s32[]{:T(128)}) fusion(bf16[512,512]{1,0:T(8,128)(2,1)S(1)} %get-tuple-element.21, s32[512]{0:T(512)S(1)} %shift_right_arithmetic.162, s32[16,512]{1,0:T(8,128)S(1)} %and.71, bf16[512,512]{1,0:T(8,128)(2,1)S(1)} %get-tuple-element.25, f32[512,512]{1,0:T(8,128)S(1)} %get-tuple-element.23, f32[]{:T(128)} %bitcast.4), kind=kLoop, calls=%fused_computation.46 | loop fusion | flops 4718589 | bytes 2131984 | tf_op jit(solution)/shard_map/reduce_sum | solution.py:93
  56.0 0.5 convolution_bitcast_fusion.1
  56.5 0.4 convolution_add_fusion.2
  57.0 1.5 %convert_multiply_fusion.1 = (f32[512,512]{1,0:T(8,128)}, f32[512,512]{1,0:T(8,128)S(1)}) fusion(bf16[512,512]{1,0:T(8,128)(2,1)S(1)} %fusion.6, f32[]{:T(128)} %bitcast.4, f32[512,512]{1,0:T(8,128)S(1)} %convolution_add_fusion.2, bf16[512,512]{1,0:T(8,128)(2,1)S(1)} %get-tuple-element.25), kind=kOutput, calls=%fused_computation.49 | convolution fusion | flops 269746176 | bytes 4194308 | tf_op jit(solution)/shard_map/dot_general | solution.py:66
  58.4 1.4 %convert_reduce_fusion.5 = (s32[]{:T(128)}, s32[]{:T(128)}, s32[]{:T(128)}) fusion(bf16[512,512]{1,0:T(8,128)(2,1)S(1)} %get-tuple-element.17, bf16[512,512]{1,0:T(8,128)(2,1)S(1)} %fusion.7, bf16[512,512]{1,0:T(8,128)(2,1)S(1)} %fusion.6, f32[512,512]{1,0:T(8,128)S(1)} %get-tuple-element.27, f32[]{:T(128)} %bitcast.4), kind=kLoop, calls=%fused_computation.47 | loop fusion | flops 2883581 | bytes 2621456 | tf_op jit(solution)/shard_map/reduce_sum | solution.py:92
  69.3 40.0 %psum.7 = s32[3]{0:T(128)} all-reduce(s32[3]{0:T(128)S(1)} %pad_add_fusion.3), channel_id=1, replica_groups=mesh['rows'=32] {'rows'}, use_global_device_ids=true, to_apply=%region_12.13 | all-reduce | flops 3 | bytes 24 | tf_op jit(solution)/shard_map/psum | solution.py:112
  109.4 2.8 %pad_maximum_fusion = f32[512,1024]{1,0:T(8,128)} fusion(f32[512,512]{1,0:T(8,128)} %get-tuple-element.22, f32[512,512]{1,0:T(8,128)S(1)} %copy-done.2), kind=kLoop, calls=%fused_computation | loop fusion | flops 524288 | bytes 4194304 | tf_op jit(solution)/shard_map/concatenate | solution.py:113
  (26 shorter events, 0.4 us)
Async XLA Ops:
  0.6 1.4 %copy-start.4 = (s32[16,512]{1,0:T(8,128)S(1)}, s32[16,512]{1,0:T(8,128)}, u32[]{:S(2)}) copy-start(s32[16,512]{1,0:T(8,128)} %param.6) | copy-start | bytes 98308
  0.6 1.4 %copy-start.5 = (s32[16,512]{1,0:T(8,128)S(1)}, s32[16,512]{1,0:T(8,128)}, u32[]{:S(2)}) copy-start(s32[16,512]{1,0:T(8,128)} %param.8) | copy-start | bytes 98308
  3.5 9.1 %collective-permute-start.1 = (s32[8,512]{1,0:T(8,128)S(1)}, s32[8,512]{1,0:T(8,128)S(1)}, u32[]{:S(2)}, u32[]{:S(2)}) collective-permute-start(s32[8,512]{1,0:T(8,128)S(1)} %fusion.25), channel_id=1, source_target_pairs={{0,31},{1,0},{2,1},{3,2},{4,3},{5,4},{6,5},{7,6},{8,7},{9,8},{10,9... | collective-permute-start | bytes 49160 | tf_op jit(solution)/shard_map/ppermute | solution.py:11
  10.3 9.1 %collective-permute-start = (s32[16,512]{1,0:T(8,128)S(1)}, s32[16,512]{1,0:T(8,128)S(1)}, u32[]{:S(2)}, u32[]{:S(2)}) collective-permute-start(s32[16,512]{1,0:T(8,128)S(1)} %get-tuple-element.9), channel_id=1, source_target_pairs={{0,1},{1,2},{2,3},{3,4},{4,5},{5,6},{6,7},{7,8},{8,9},{9,10},{10,1... | collective-permute-start | bytes 98312 | tf_op jit(solution)/shard_map/ppermute | solution.py:11
  19.4 8.0 %collective-permute-start.4 = (s32[16,512]{1,0:T(8,128)S(1)}, s32[16,512]{1,0:T(8,128)S(1)}, u32[]{:S(2)}, u32[]{:S(2)}) collective-permute-start(s32[16,512]{1,0:T(8,128)S(1)} %get-tuple-element.20), channel_id=1, source_target_pairs={{0,1},{1,2},{2,3},{3,4},{4,5},{5,6},{6,7},{7,8},{8,9},{9,10},{10,1... | collective-permute-start | bytes 98312 | tf_op jit(solution)/shard_map/ppermute | solution.py:11
  22.0 9.8 %collective-permute-start.2 = (s32[8,512]{1,0:T(8,128)S(1)}, s32[8,512]{1,0:T(8,128)S(1)}, u32[]{:S(2)}, u32[]{:S(2)}) collective-permute-start(s32[8,512]{1,0:T(8,128)S(1)} %fusion.24), channel_id=1, source_target_pairs={{0,31},{1,0},{2,1},{3,2},{4,3},{5,4},{6,5},{7,6},{8,7},{9,8},{10,9... | collective-permute-start | bytes 49160 | tf_op jit(solution)/shard_map/ppermute | solution.py:11
  29.8 2.0 %collective-permute-start.5 = (s32[8,512]{1,0:T(8,128)S(1)}, s32[8,512]{1,0:T(8,128)S(1)}, u32[]{:S(2)}, u32[]{:S(2)}) collective-permute-start(s32[8,512]{1,0:T(8,128)S(1)} %fusion.23), channel_id=1, source_target_pairs={{0,31},{1,0},{2,1},{3,2},{4,3},{5,4},{6,5},{7,6},{8,7},{9,8},{10,9... | collective-permute-start | bytes 49160 | tf_op jit(solution)/shard_map/ppermute | solution.py:11
  33.2 5.0 %copy-start.1 = (s32[256,512]{1,0:T(8,128)}, s32[256,512]{1,0:T(8,128)S(1)}, u32[]{:S(2)}) copy-start(s32[256,512]{1,0:T(8,128)S(1)} %get-tuple-element.19) | copy-start | bytes 1572868
  43.1 12.9 %collective-permute-start.3 = (s32[16,512]{1,0:T(8,128)S(1)}, s32[16,512]{1,0:T(8,128)S(1)}, u32[]{:S(2)}, u32[]{:S(2)}) collective-permute-start(s32[16,512]{1,0:T(8,128)S(1)} %get-tuple-element.24), channel_id=1, source_target_pairs={{0,1},{1,2},{2,3},{3,4},{4,5},{5,6},{6,7},{7,8},{8,9},{9,10},{10,1... | collective-permute-start | bytes 98312 | tf_op jit(solution)/shard_map/ppermute | solution.py:11
  51.6 1.0 copy-start
  51.6 1.4 %copy-start.3 = (s32[512,512]{0,1:T(8,128)S(1)}, s32[512,512]{0,1:T(8,128)}, u32[]{:S(2)}) copy-start(s32[512,512]{0,1:T(8,128)} %copy.13) | copy-start | bytes 3145732
  58.4 50.9 %copy-start.2 = (f32[512,512]{1,0:T(8,128)S(1)}, f32[512,512]{1,0:T(8,128)}, u32[]{:S(2)}) copy-start(f32[512,512]{1,0:T(8,128)} %get-tuple-element.26) | copy-start | bytes 3145732
where the time goes:
time: 113 us; the launch traced here: 112 us
  blocking collectives  40 us (35%)
  local copies, waits for them, and re-layouts  20.4 us (18%)
  matrix products  14.6 us (13%)
  other arithmetic  13.6 us (12%)
  starting transfers between devices  12.5 us (11%)
  between operations  11 us (10%)
    psum x1, blocking collectives, on_device(): stacked = lax.psum(stacked, 'rows')  40 us
    ppermute x6, starting transfers between devices, shifted(): lax.ppermute(array, axis, [(i, (i + by) % count) for i in range(count)])  12.5 us
    rev x3, local copies, waits for them, and re-layouts, unfold_within(): jnp.where(col_ids < row_ids, folded, jnp.zeros_like(folded))[::-1, ::-1]  8.42 us
    concatenate x3, local copies, waits for them, and re-layouts, unfold_within(): upper_half = jnp.concatenate([top_rows, bottom_rows], axis=0)  7.69 us
    dot_general x3, matrix products, support_across(): jnp.dot(across, next_within, preferred_element_type=jnp.float32)  6.13 us
    concatenate x3, other arithmetic, unfold_within(): upper_half = jnp.concatenate([top_rows, bottom_rows], axis=0)  4.27 us
    dot_general x3, matrix products, support_across(): between = jnp.dot(within, across, preferred_element_type=jnp.float32)  3.25 us
    concatenate x1, other arithmetic, on_device(): jnp.concatenate([inside * within.astype(jnp.float32), between * across.as...  2.76 us
  transfers between devices with their start and end apart: 6, of which 0 were waited for; matrix products, arithmetic and copies ran while one was open for 24% of the time, Pallas kernels for 0%

commit v1 on v0

v1 whole, which is shorter than its diff:
```python
import functools

import jax
import jax.numpy as jnp
from jax import lax
from jax.experimental import pallas as pl
from jax.experimental.pallas import tpu as pltpu
from jax.sharding import PartitionSpec as P

F8 = jnp.float8_e4m3fn
F32 = jnp.float32
WORD = 32


def dot_nt(lhs, rhs):
    return lax.dot_general(lhs, rhs, (((1,), (1,)), ((), ())), preferred_element_type=F32)


def send(src, dst, send_sem, recv_sem, target):
    return pltpu.make_async_remote_copy(
        src_ref=src,
        dst_ref=dst,
        send_sem=send_sem,
        recv_sem=recv_sem,
        device_id=(target,),
        device_id_type=pl.DeviceIdType.MESH,
    )


def kernel(
    n, k_ref, ad_ref, ar_ref, ld_ref, lr_ref, out_ref, cnt_ref,
    own, halo, x, eye, tri, psum_in, psum_next, psum_btw, mine, gathered,
    send_sems, recv_sems, cnt_send, cnt_recv,
):
    t = ad_ref.shape[1]
    words = ad_ref.shape[0]
    me = lax.axis_index("rows")
    barrier = pltpu.get_barrier_semaphore()

    def greet(d, carry):
        pl.semaphore_signal(
            barrier, inc=1, device_id=(lax.rem(me + d, n),), device_id_type=pl.DeviceIdType.MESH
        )
        return carry

    lax.fori_loop(1, n, greet, 0)
    own[0] = ad_ref[...] & ld_ref[...]
    own[1] = ar_ref[...] & lr_ref[...]

    AT, W, A = (pl.ds(i * t, t) for i in range(3))
    shift = lax.broadcasted_iota(jnp.int32, (WORD, t), 0)
    col = lax.broadcasted_iota(jnp.int32, (WORD, t), 1)

    def unpack(src, upper):
        dst = []
        for w in range(words):
            bits = (jnp.broadcast_to(src[w : w + 1, :], (WORD, t)) >> shift) & 1
            if upper:
                bits = jnp.where(col - shift > WORD * w, bits, 0)
            dst.append(bits.astype(F32).astype(F8))
        return dst

    def put_across(src, j):
        for w, rows in enumerate(unpack(src, False)):
            x[j, pl.ds(WORD * w, WORD), A] = rows

    def put_transposed(j):
        x[j + 1, :, AT] = dot_nt(eye[...], x[j, :, A]).astype(F8)

    def put_within(src, j):
        for w, rows in enumerate(unpack(src, True)):
            tri[pl.ds(WORD * w, WORD), :] = rows
        flipped = dot_nt(eye[...], tri[...])
        x[j, :, W] = (flipped + tri[...].astype(F32)).astype(F8)

    row_id = lax.broadcasted_iota(jnp.int32, (t, t), 0)
    col_id = lax.broadcasted_iota(jnp.int32, (t, t), 1)
    eye[...] = jnp.where(row_id == col_id, 1.0, 0.0).astype(F32).astype(F8)
    put_across(own.at[1], 1)

    pl.semaphore_wait(barrier, n - 1)
    routes = ((1, 2, 1), (0, 1, 1), (0, 3, -1), (1, 4, -1), (1, 0, 2), (0, 5, -2))
    copies = {}
    for what, slot, by in routes:
        copies[slot] = send(
            own.at[what], halo.at[slot], send_sems.at[slot], recv_sems.at[slot],
            lax.rem(me + by + n, n),
        )
        copies[slot].start()

    thresh = (k_ref[0] - 2).astype(F32)

    put_within(own.at[0], 1)
    put_transposed(1)
    psum_in[...] = dot_nt(x[1, :, t:], x[1, :, t:])
    psum_next[...] = dot_nt(x[2, :, AT], x[2, :, AT])
    psum_btw[...] = dot_nt(x[1, :, W], x[2, :, AT])

    def total(values):
        lanes = jnp.sum(values, axis=0, keepdims=True)
        return sum(lanes[:, i : i + 128] for i in range(0, t, 128))

    def keep(support, j, part):
        old = x[j, :, part].astype(F32)
        return old, jnp.where(support >= thresh, old, 0.0)

    def inside(j):
        return dot_nt(x[j], x[j])

    def between(j):
        return dot_nt(x[j, :, t:], x[j + 1, :, : 2 * t])

    copies[2].wait_recv()
    put_across(halo.at[2], 0)
    put_transposed(0)
    copies[1].wait_recv()
    put_within(halo.at[1], 0)
    copies[3].wait_recv()
    put_within(halo.at[3], 2)
    copies[4].wait_recv()
    put_across(halo.at[4], 2)
    put_transposed(2)
    copies[0].wait_recv()
    for w, rows in enumerate(unpack(halo.at[0], False)):
        tri[pl.ds(WORD * w, WORD), :] = rows
    x[0, :, AT] = dot_nt(eye[...], tri[...]).astype(F8)
    copies[5].wait_recv()
    put_within(halo.at[5], 3)

    counts = []

    def own_count(old_w, new_w, old_a, new_a):
        counts.append(total((old_w - new_w) + 2.0 * (old_a - new_a)))

    _, wm = keep(inside(0), 0, W)
    _, am = keep(between(0), 0, A)
    old_w, w0 = keep(psum_in[...] + dot_nt(x[1, :, AT], x[1, :, AT]), 1, W)
    old_a, a0 = keep(psum_btw[...] + dot_nt(x[1, :, A], x[2, :, W]), 1, A)
    own_count(old_w, w0, old_a, a0)
    _, w1 = keep(psum_next[...] + dot_nt(x[2, :, t:], x[2, :, t:]), 2, W)
    _, a1 = keep(between(2), 2, A)
    x[0, :, W] = wm.astype(F8)
    x[0, :, A] = am.astype(F8)
    x[1, :, W] = w0.astype(F8)
    x[1, :, A] = a0.astype(F8)
    x[2, :, W] = w1.astype(F8)
    x[2, :, A] = a1.astype(F8)
    put_transposed(0)
    put_transposed(1)

    _, am = keep(between(0), 0, A)
    old_w, w0 = keep(inside(1), 1, W)
    old_a, a0 = keep(between(1), 1, A)
    own_count(old_w, w0, old_a, a0)
    _, w1 = keep(inside(2), 2, W)
    x[0, :, A] = am.astype(F8)
    x[1, :, W] = w0.astype(F8)
    x[1, :, A] = a0.astype(F8)
    x[2, :, W] = w1.astype(F8)
    put_transposed(0)
    put_transposed(1)

    support_w = inside(1)
    old_w, w0 = keep(support_w, 1, W)
    support_a = between(1)
    old_a, a0 = keep(support_a, 1, A)
    own_count(old_w, w0, old_a, a0)
    mine[...] = jnp.zeros_like(mine)
    for step, row in enumerate(counts):
        mine[step : step + 1, :] = row.astype(jnp.int32)

    def share(d, carry):
        send(mine, gathered.at[d - 1], cnt_send, cnt_recv, lax.rem(me + d, n)).start()
        return carry

    lax.fori_loop(1, n, share, 0)
    out_ref[:, :t] = support_w * w0
    out_ref[:, t:] = support_a * a0
    for slot in range(6):
        copies[slot].wait_send()
    pltpu.make_async_copy(gathered, gathered, cnt_recv).wait()
    summed = mine[...] + jnp.sum(gathered[...], axis=0)
    for step in range(cnt_ref.shape[0]):
        cnt_ref[step] = jnp.sum(summed[step : step + 1, :]) // 2
    pltpu.make_async_copy(gathered, gathered, cnt_send).wait()


def on_device(n, adj_diag, adj_right, alive_diag, alive_right, truss_k):
    words, t = adj_diag.shape
    vmem = pl.BlockSpec(memory_space=pltpu.VMEM)
    smem = pl.BlockSpec(memory_space=pltpu.SMEM)
    return pl.pallas_call(
        functools.partial(kernel, n),
        out_shape=(
            jax.ShapeDtypeStruct((t, 2 * t), F32),
            jax.ShapeDtypeStruct((3,), jnp.int32),
        ),
        in_specs=[smem] + [vmem] * 4,
        out_specs=(vmem, smem),
        scratch_shapes=[
            pltpu.VMEM((2, words, t), jnp.int32),
            pltpu.VMEM((6, words, t), jnp.int32),
            pltpu.VMEM((4, t, 3 * t), F8),
            pltpu.VMEM((t, t), F8),
            pltpu.VMEM((t, t), F8),
            pltpu.VMEM((t, t), F32),
            pltpu.VMEM((t, t), F32),
            pltpu.VMEM((t, t), F32),
            pltpu.VMEM((8, 128), jnp.int32),
            pltpu.VMEM((n - 1, 8, 128), jnp.int32),
            pltpu.SemaphoreType.DMA((6,)),
            pltpu.SemaphoreType.DMA((6,)),
            pltpu.SemaphoreType.DMA,
            pltpu.SemaphoreType.DMA,
        ],
        compiler_params=pltpu.CompilerParams(collective_id=0, has_side_effects=True),
    )(truss_k, adj_diag, adj_right, alive_diag, alive_right)


def solution(mesh):
    row = P("rows", None)
    return jax.shard_map(
        functools.partial(on_device, mesh.shape["rows"]),
        mesh=mesh,
        in_specs=(row, row, row, row, P()),
        out_specs=(row, P()),
        check_vma=False,
    )
```

time: 113 us -> 29.3 us (0.26)
  blocking collectives: 40 us -> 0 us
  Pallas kernels: 0 us -> 24.1 us
  local copies, waits for them, and re-layouts: 20.4 us -> 3.68 us
  matrix products: 14.6 us -> 0 us
  other arithmetic: 13.6 us -> 0 us
  starting transfers between devices: 12.5 us -> 0 us
  between operations: 11 us -> 1.29 us
    psum x1 -> x0, blocking collectives: 40 us -> none  [on_device(): stacked = lax.psum(stacked, 'rows')]
    pallas_call x0 -> x1, Pallas kernels: none -> 24.1 us  [on_device(): pl.pallas_call(functools.partial(kernel, n), out_shape=(jax.ShapeDtypeStr...]
    dot_general x15 -> x0, matrix products: 14.6 us -> none  [the longest x3 6.13 us: support_across(): jnp.dot(across, next_within, preferred_element_type=jnp.float32)]
    ppermute x6 -> x0, starting transfers between devices: 12.5 us -> none  [shifted(): lax.ppermute(array, axis, [(i, (i + by) % count) for i in range(count)])]
    rev x6 -> x0, local copies, waits for them, and re-layouts: 11.1 us -> none  [the longest x3 8.42 us: unfold_within(): jnp.where(col_ids < row_ids, folded, jnp.zeros_like(folded))[::-1, ::-1]]
    concatenate x3 -> x0, local copies, waits for them, and re-layouts: 7.69 us -> none  [unfold_within(): upper_half = jnp.concatenate([top_rows, bottom_rows], axis=0)]
    concatenate x4 -> x0, other arithmetic: 7.04 us -> none  [the longest x3 4.27 us: unfold_within(): upper_half = jnp.concatenate([top_rows, bottom_rows], axis=0)]
    reduce_sum x5 -> x0, other arithmetic: 3.26 us -> none  [the longest x1 1.48 us: tally(): removed = removed + jnp.sum((across - new_across).astype(jnp.int32))]
  transfers between devices with their start and end apart: 6 -> 0, of which waited for: 0 -> 0; matrix products, arithmetic and copies ran while one was open for 24% -> 0% of each run, Pallas kernels for 0% -> 0%
where the time goes in v1:
time: 29.3 us; the launch traced here: 29.1 us
  Pallas kernels  24.1 us (82%)
  local copies, waits for them, and re-layouts  3.68 us (13%)
  between operations  1.29 us (4%)
    pallas_call x1, Pallas kernels, on_device(): pl.pallas_call(functools.partial(kernel, n), out_shape=(jax.ShapeDtypeStr...  24.1 us
    unnamed x4, local copies, waits for them, and re-layouts  3.68 us

profile of v1, /device:TPU:0, one launch (start us, length us, event | category | flops | bytes accessed | tf_op | source)
XLA Modules:
  0.0 29.1 jit_solution(1070310922929560355)
XLA Ops:
  1.3 24.1 %shard_map.68 = (f32[512,1024]{1,0:T(8,128)}, s32[3]{0:T(128)}) custom-call(s32[1]{0:T(128)S(6)} %copy.9.k_ref, s32[16,512]{1,0:T(8,128)} %ad_ref.1, s32[16,512]{1,0:T(8,128)} %ar_ref.1, s32[16,512]{1,0:T(8,128)} %ld_ref.1, s32[16,512]{1,0:T(8,128)} %lr_ref.1), custom_call_target="tpu_custom_call" | custom-call | tf_op jit(solution)/shard_map/pallas_call | solution.py:192
  25.4 0.0 copy-start
  25.4 3.2 %copy.10 = f32[512,1024]{1,0:T(8,128)} copy(f32[512,1024]{1,0:T(8,128)} %get-tuple-element.4) | data formatting | bytes 4194304
  28.6 0.0 copy-done
  28.6 0.5 %copy.11 = s32[3]{0:T(128)} copy(s32[3]{0:T(128)S(1)} %copy-done) | data formatting | bytes 24
Async XLA Ops:
  25.4 3.2 %copy-start = (s32[3]{0:T(128)S(1)}, s32[3]{0:T(128)}, u32[]{:S(2)}) copy-start(s32[3]{0:T(128)} %get-tuple-element.5) | copy-start | bytes 40

commit v2 on v1

v2 whole, which is shorter than its diff:
```python
import functools

import jax
import jax.numpy as jnp
from jax import lax
from jax.experimental import pallas as pl
from jax.experimental.pallas import tpu as pltpu
from jax.sharding import PartitionSpec as P

F8 = jnp.float8_e4m3fn
F32 = jnp.float32
WORD = 32


def dot_nt(lhs, rhs):
    return lax.dot_general(lhs, rhs, (((1,), (1,)), ((), ())), preferred_element_type=F32)


def send(src, dst, send_sem, recv_sem, target):
    return pltpu.make_async_remote_copy(
        src_ref=src,
        dst_ref=dst,
        send_sem=send_sem,
        recv_sem=recv_sem,
        device_id=(target,),
        device_id_type=pl.DeviceIdType.MESH,
    )


def kernel(
    n, k_ref, ad_ref, ar_ref, ld_ref, lr_ref, out_ref, cnt_ref,
    raw, own, halo, x, eye, tri, spare, psum_in, psum_next, psum_btw, mine, gathered,
    raw_sems, send_sems, recv_sems, relay_sems, cnt_send, cnt_recv,
):
    t = ad_ref.shape[1]
    words = ad_ref.shape[0]
    me = lax.axis_index("rows")
    even = lax.rem(me, 2) == 0
    loads = [
        pltpu.make_async_copy(src, raw.at[i], raw_sems.at[i])
        for i, src in enumerate((ad_ref, ar_ref, ld_ref, lr_ref))
    ]
    for load in loads:
        load.start()
    barrier = pltpu.get_barrier_semaphore()

    def greet(d, carry):
        pl.semaphore_signal(
            barrier, inc=1, device_id=(lax.rem(me + d, n),), device_id_type=pl.DeviceIdType.MESH
        )
        return carry

    lax.fori_loop(1, n, greet, 0)
    for load in loads:
        load.wait()
    own[0] = raw[0] & raw[2]
    own[1] = raw[1] & raw[3]

    AT, W, A = (pl.ds(i * t, t) for i in range(3))
    shift = lax.broadcasted_iota(jnp.int32, (WORD, t), 0)
    col = lax.broadcasted_iota(jnp.int32, (WORD, t), 1)

    half = t // 2

    def unpack(src, upper):
        for w in range(words):
            left = half if upper and 2 * w >= words else 0
            bits = (jnp.broadcast_to(src[w : w + 1, left:], (WORD, t - left)) >> shift[:, left:]) & 1
            if upper:
                bits = jnp.where(col[:, left:] - shift[:, left:] > WORD * w, bits, 0)
            yield pl.ds(WORD * w, WORD), pl.ds(left, t - left), bits.astype(F32).astype(F8)

    def put_across(src, j):
        for rows, _, bits in unpack(src, False):
            x[j, rows, A] = bits

    def put_transposed(j):
        x[j + 1, :, AT] = dot_nt(eye[...], x[j, :, A]).astype(F8)

    def put_within(src, j):
        for rows, cols, bits in unpack(src, True):
            tri[rows, cols] = bits
        flipped = dot_nt(eye[...], tri[...])
        x[j, :, W] = (flipped + tri[...].astype(F32)).astype(F8)

    row_id = lax.broadcasted_iota(jnp.int32, (t, t), 0)
    col_id = lax.broadcasted_iota(jnp.int32, (t, t), 1)
    eye[...] = jnp.where(row_id == col_id, 1.0, 0.0).astype(F32).astype(F8)
    tri[half:, :half] = jnp.zeros((t - half, half), F32).astype(F8)
    put_across(own.at[1], 1)

    pl.semaphore_wait(barrier, n - 1)
    top, low = pl.ds(0, words // 2), pl.ds(words // 2, words // 2)
    whole, right = pl.ds(0, t), pl.ds(half, half)

    def pieces(source, slot, by, sends):
        parts = [(top, whole), (low, right if slot in (1, 3, 5) else whole)]
        return [
            send(
                source.at[rows, cols], halo.at[slot, rows, cols],
                sends.at[i], recv_sems.at[2 * slot + i], lax.rem(me + by + n, n),
            )
            for i, (rows, cols) in enumerate(parts)
        ]

    def start(slot):
        for piece in copies[slot]:
            piece.start()

    def arrive(slot):
        for piece in copies[slot]:
            piece.wait_recv()

    def left(copy):
        for piece in copy:
            piece.wait_send()

    routes = {2: (1, 1), 3: (0, -1), 1: (0, 1), 4: (1, -1), 0: (1, 2), 5: (0, -2)}
    copies = {
        slot: pieces(own.at[what], slot, by, send_sems.at[slot])
        for slot, (what, by) in routes.items()
    }
    to_right = pieces(halo.at[2], 0, 1, relay_sems)
    to_left = pieces(halo.at[3], 5, -1, relay_sems)
    start(2)
    start(3)

    @pl.when(even)
    def _():
        start(0)

    @pl.when(jnp.logical_not(even))
    def _():
        start(5)

    start(1)
    start(4)

    thresh = (k_ref[0] - 2).astype(F32)

    put_within(own.at[0], 1)
    put_transposed(1)
    psum_in[...] = dot_nt(x[1, :, t:], x[1, :, t:])
    psum_next[...] = dot_nt(x[2, :, AT], x[2, :, AT])
    psum_btw[...] = dot_nt(x[1, :, W], x[2, :, AT])

    def total(values):
        lanes = jnp.sum(values, axis=0, keepdims=True)
        return sum(lanes[:, i : i + 128] for i in range(0, t, 128))

    def keep(support, j, part):
        old = x[j, :, part].astype(F32)
        return old, jnp.where(support >= thresh, old, 0.0)

    def inside(j):
        return dot_nt(x[j], x[j])

    def between(j):
        return dot_nt(x[j, :, t:], x[j + 1, :, : 2 * t])

    arrive(2)

    @pl.when(even)
    def _():
        for piece in to_right:
            piece.start()

    arrive(3)

    @pl.when(jnp.logical_not(even))
    def _():
        for piece in to_left:
            piece.start()

    put_across(halo.at[2], 0)
    put_transposed(0)
    put_within(halo.at[3], 2)

    counts = []

    def own_count(old_w, new_w, old_a, new_a):
        counts.append(total((old_w - new_w) + 2.0 * (old_a - new_a)))

    old_w, w0 = keep(psum_in[...] + dot_nt(x[1, :, AT], x[1, :, AT]), 1, W)
    old_a, a0 = keep(psum_btw[...] + dot_nt(x[1, :, A], x[2, :, W]), 1, A)
    own_count(old_w, w0, old_a, a0)
    arrive(1)
    put_within(halo.at[1], 0)
    arrive(4)
    put_across(halo.at[4], 2)
    put_transposed(2)
    _, am = keep(between(0), 0, A)
    _, w1 = keep(psum_next[...] + dot_nt(x[2, :, t:], x[2, :, t:]), 2, W)
    arrive(0)
    for rows, _, bits in unpack(halo.at[0], False):
        spare[rows, :] = bits
    x[0, :, AT] = dot_nt(eye[...], spare[...]).astype(F8)
    _, wm = keep(inside(0), 0, W)
    arrive(5)
    put_within(halo.at[5], 3)
    _, a1 = keep(between(2), 2, A)
    x[0, :, W] = wm.astype(F8)
    x[0, :, A] = am.astype(F8)
    x[1, :, W] = w0.astype(F8)
    x[1, :, A] = a0.astype(F8)
    x[2, :, W] = w1.astype(F8)
    x[2, :, A] = a1.astype(F8)
    put_transposed(0)
    put_transposed(1)

    _, am = keep(between(0), 0, A)
    old_w, w0 = keep(inside(1), 1, W)
    old_a, a0 = keep(between(1), 1, A)
    own_count(old_w, w0, old_a, a0)
    _, w1 = keep(inside(2), 2, W)
    x[0, :, A] = am.astype(F8)
    x[1, :, W] = w0.astype(F8)
    x[1, :, A] = a0.astype(F8)
    x[2, :, W] = w1.astype(F8)
    put_transposed(0)
    put_transposed(1)

    support_w = inside(1)
    old_w, w0 = keep(support_w, 1, W)
    support_a = between(1)
    old_a, a0 = keep(support_a, 1, A)
    own_count(old_w, w0, old_a, a0)
    lane = lax.broadcasted_iota(jnp.int32, (1, 128), 1)
    packed = jnp.zeros((1, 128), F32)
    for step, row in enumerate(counts):
        packed = jnp.where(lane == step, jnp.sum(row, axis=1, keepdims=True), packed)
    mine[...] = packed.astype(jnp.int32)

    def share(d, carry):
        send(mine, gathered.at[d - 1], cnt_send, cnt_recv, lax.rem(me + d, n)).start()
        return carry

    lax.fori_loop(1, n, share, 0)
    out_ref[:, :t] = support_w * w0
    out_ref[:, t:] = support_a * a0
    for slot in range(1, 5):
        left(copies[slot])

    @pl.when(even)
    def _():
        left(copies[0])
        left(to_right)

    @pl.when(jnp.logical_not(even))
    def _():
        left(copies[5])
        left(to_left)

    pltpu.make_async_copy(gathered, gathered, cnt_recv).wait()
    summed = mine[...] + jnp.sum(gathered[...], axis=0)
    for step in range(cnt_ref.shape[0]):
        cnt_ref[step] = jnp.sum(jnp.where(lane == step, summed, 0)) // 2
    pltpu.make_async_copy(gathered, gathered, cnt_send).wait()


def on_device(n, adj_diag, adj_right, alive_diag, alive_right, truss_k):
    words, t = adj_diag.shape
    vmem = pl.BlockSpec(memory_space=pltpu.VMEM)
    smem = pl.BlockSpec(memory_space=pltpu.SMEM)
    return pl.pallas_call(
        functools.partial(kernel, n),
        out_shape=(
            jax.ShapeDtypeStruct((t, 2 * t), F32),
            jax.ShapeDtypeStruct((3,), jnp.int32),
        ),
        in_specs=[smem] + [pl.BlockSpec(memory_space=pltpu.MemorySpace.HBM)] * 4,
        out_specs=(vmem, smem),
        scratch_shapes=[
            pltpu.VMEM((4, words, t), jnp.int32),
            pltpu.VMEM((2, words, t), jnp.int32),
            pltpu.VMEM((6, words, t), jnp.int32),
            pltpu.VMEM((4, t, 3 * t), F8),
            pltpu.VMEM((t, t), F8),
            pltpu.VMEM((t, t), F8),
            pltpu.VMEM((t, t), F8),
            pltpu.VMEM((t, t), F32),
            pltpu.VMEM((t, t), F32),
            pltpu.VMEM((t, t), F32),
            pltpu.VMEM((1, 128), jnp.int32),
            pltpu.VMEM((n - 1, 1, 128), jnp.int32),
            pltpu.SemaphoreType.DMA((4,)),
            pltpu.SemaphoreType.DMA((6, 2)),
            pltpu.SemaphoreType.DMA((12,)),
            pltpu.SemaphoreType.DMA((2,)),
            pltpu.SemaphoreType.DMA,
            pltpu.SemaphoreType.DMA,
        ],
        compiler_params=pltpu.CompilerParams(collective_id=0, has_side_effects=True, vmem_limit_bytes=24 * 2**20),
    )(truss_k, *[pltpu.with_memory_space_constraint(v, pltpu.HBM) for v in (adj_diag, adj_right, alive_diag, alive_right)])


def solution(mesh):
    row = P("rows", None)
    return jax.shard_map(
        functools.partial(on_device, mesh.shape["rows"]),
        mesh=mesh,
        in_specs=(row, row, row, row, P()),
        out_specs=(row, P()),
        check_vma=False,
    )
```

time: 29.3 us -> 26.4 us (0.901)
  local copies, waits for them, and re-layouts: 3.68 us -> 1.83 us
  Pallas kernels: 24.1 us -> 23.1 us
    unnamed x4 -> x2, local copies, waits for them, and re-layouts: 3.68 us -> 1.83 us
    pallas_call x1, Pallas kernels: 24.1 us -> 23.1 us  [on_device(): pl.pallas_call(functools.partial(kernel, n), out_shape=(jax.ShapeDtypeStr...]
where the time goes in v2:
time: 26.4 us; the launch traced here: 26.2 us
  Pallas kernels  23.1 us (88%)
  local copies, waits for them, and re-layouts  1.83 us (7%)
  between operations  1.29 us (5%)
    pallas_call x1, Pallas kernels, on_device(): pl.pallas_call(functools.partial(kernel, n), out_shape=(jax.ShapeDtypeStr...  23.1 us
    unnamed x2, local copies, waits for them, and re-layouts  1.83 us

profile of v2, /device:TPU:0, one launch (start us, length us, event | category | flops | bytes accessed | tf_op | source)
XLA Modules:
  0.0 26.2 jit_solution(13590079979680012348)
XLA Ops:
  1.3 23.1 %shard_map.68 = (f32[512,1024]{1,0:T(8,128)S(1)}, s32[3]{0:T(128)S(1)}) custom-call(s32[1]{0:T(128)S(6)} %copy.9.k_ref, s32[16,512]{1,0:T(8,128)} %ad_ref.1, s32[16,512]{1,0:T(8,128)} %ar_ref.1, s32[16,512]{1,0:T(8,128)} %ld_ref.1, s32[16,512]{1,0:T(8,128)} %lr_ref.1), custom_call_target="tpu_custom_call" | custom-call | tf_op jit(solution)/shard_map/pallas_call | solution.py:265
  24.4 1.3 %copy.10 = f32[512,1024]{1,0:T(8,128)} copy(f32[512,1024]{1,0:T(8,128)S(1)} %get-tuple-element.4) | data formatting | bytes 4194304
  25.7 0.5 %copy.11 = s32[3]{0:T(128)} copy(s32[3]{0:T(128)S(1)} %get-tuple-element.5) | data formatting | bytes 24

commit v3 on v2

--- a/solution.py
+++ b/solution.py
@@ -10,6 +10,7 @@
 F8 = jnp.float8_e4m3fn
 F32 = jnp.float32
 WORD = 32
+ITERS = 3
 
 
 def dot_nt(lhs, rhs):
@@ -29,28 +30,30 @@
 
 def kernel(
     n, k_ref, ad_ref, ar_ref, ld_ref, lr_ref, out_ref, cnt_ref,
-    raw, own, halo, x, eye, tri, spare, psum_in, psum_next, psum_btw, mine, gathered,
-    raw_sems, send_sems, recv_sems, relay_sems, cnt_send, cnt_recv,
+    k_smem, raw, own, halo, x, eye, tri, spare, psum_in, psum_next, psum_btw, mine, gathered,
+    k_sem, raw_sems, send_sems, recv_sems, relay_sems, cnt_send, cnt_recv,
 ):
     t = ad_ref.shape[1]
     words = ad_ref.shape[0]
     me = lax.axis_index("rows")
     even = lax.rem(me, 2) == 0
+    barrier = pltpu.get_barrier_semaphore()
+
+    def greet(d, carry):
+        pl.semaphore_signal(
+            barrier, inc=1, device_id=(lax.rem(me + d, n),), device_id_type=pl.DeviceIdType.MESH
+        )
+        return carry
+
+    lax.fori_loop(1, n, greet, 0)
     loads = [
         pltpu.make_async_copy(src, raw.at[i], raw_sems.at[i])
         for i, src in enumerate((ad_ref, ar_ref, ld_ref, lr_ref))
     ]
     for load in loads:
         load.start()
-    barrier = pltpu.get_barrier_semaphore()
-
-    def greet(d, carry):
-        pl.semaphore_signal(
-            barrier, inc=1, device_id=(lax.rem(me + d, n),), device_id_type=pl.DeviceIdType.MESH
-        )
-        return carry
-
-    lax.fori_loop(1, n, greet, 0)
+    k_load = pltpu.make_async_copy(k_ref, k_smem, k_sem)
+    k_load.start()
     for load in loads:
         load.wait()
     own[0] = raw[0] & raw[2]
@@ -87,7 +90,6 @@
     col_id = lax.broadcasted_iota(jnp.int32, (t, t), 1)
     eye[...] = jnp.where(row_id == col_id, 1.0, 0.0).astype(F32).astype(F8)
     tri[half:, :half] = jnp.zeros((t - half, half), F32).astype(F8)
-    put_across(own.at[1], 1)
 
     pl.semaphore_wait(barrier, n - 1)
     top, low = pl.ds(0, words // 2), pl.ds(words // 2, words // 2)
@@ -122,8 +124,8 @@
     }
     to_right = pieces(halo.at[2], 0, 1, relay_sems)
     to_left = pieces(halo.at[3], 5, -1, relay_sems)
+    start(3)
     start(2)
-    start(3)
 
     @pl.when(even)
     def _():
@@ -133,10 +135,12 @@
     def _():
         start(5)
 
+    start(4)
     start(1)
-    start(4)
-
-    thresh = (k_ref[0] - 2).astype(F32)
+    put_across(own.at[1], 1)
+
+    k_load.wait()
+    thresh = (k_smem[0] - 2).astype(F32)
 
     put_within(own.at[0], 1)
     put_transposed(1)
@@ -158,6 +162,11 @@
     def between(j):
         return dot_nt(x[j, :, t:], x[j + 1, :, : 2 * t])
 
+    counts = []
+
+    def own_count(old_w, new_w, old_a, new_a):
+        counts.append(total((old_w - new_w) + 2.0 * (old_a - new_a)))
+
     arrive(2)
 
     @pl.when(even)
@@ -165,6 +174,12 @@
         for piece in to_right:
             piece.start()
 
+    put_across(halo.at[2], 0)
+    put_transposed(0)
+    old_w, w0 = keep(psum_in[...] + dot_nt(x[1, :, AT], x[1, :, AT]), 1, W)
+    arrive(1)
+    put_within(halo.at[1], 0)
+    _, am = keep(between(0), 0, A)
     arrive(3)
 
     @pl.when(jnp.logical_not(even))
@@ -172,30 +187,18 @@
         for piece in to_left:
             piece.start()
 
-    put_across(halo.at[2], 0)
-    put_transposed(0)
-    put_within(halo.at[3], 2)
-
-    counts = []
-
-    def own_count(old_w, new_w, old_a, new_a):
-        counts.append(total((old_w - new_w) + 2.0 * (old_a - new_a)))
-
-    old_w, w0 = keep(psum_in[...] + dot_nt(x[1, :, AT], x[1, :, AT]), 1, W)
-    old_a, a0 = keep(psum_btw[...] + dot_nt(x[1, :, A], x[2, :, W]), 1, A)
-    own_count(old_w, w0, old_a, a0)
-    arrive(1)
-    put_within(halo.at[1], 0)
-    arrive(4)
-    put_across(halo.at[4], 2)
-    put_transposed(2)
-    _, am = keep(between(0), 0, A)
-    _, w1 = keep(psum_next[...] + dot_nt(x[2, :, t:], x[2, :, t:]), 2, W)
     arrive(0)
     for rows, _, bits in unpack(halo.at[0], False):
         spare[rows, :] = bits
     x[0, :, AT] = dot_nt(eye[...], spare[...]).astype(F8)
     _, wm = keep(inside(0), 0, W)
+    put_within(halo.at[3], 2)
+    old_a, a0 = keep(psum_btw[...] + dot_nt(x[1, :, A], x[2, :, W]), 1, A)
+    own_count(old_w, w0, old_a, a0)
+    arrive(4)
+    put_across(halo.at[4], 2)
+    put_transposed(2)
+    _, w1 = keep(psum_next[...] + dot_nt(x[2, :, t:], x[2, :, t:]), 2, W)
     arrive(5)
     put_within(halo.at[5], 3)
     _, a1 = keep(between(2), 2, A)
@@ -252,25 +255,49 @@
         left(to_left)
 
     pltpu.make_async_copy(gathered, gathered, cnt_recv).wait()
-    summed = mine[...] + jnp.sum(gathered[...], axis=0)
-    for step in range(cnt_ref.shape[0]):
-        cnt_ref[step] = jnp.sum(jnp.where(lane == step, summed, 0)) // 2
+    cnt_ref[: n - 1] = gathered[...]
+    cnt_ref[n - 1] = mine[...]
     pltpu.make_async_copy(gathered, gathered, cnt_send).wait()
+
+
+def finish(support_ref, cnt_ref, out_ref, removed_ref, sems):
+    parts = sems.shape[0]
+    rows = support_ref.shape[0] // parts
+    copies = [
+        pltpu.make_async_copy(
+            support_ref.at[pl.ds(i * rows, rows)], out_ref.at[pl.ds(i * rows, rows)], sems.at[i]
+        )
+        for i in range(parts)
+    ]
+    for copy in copies:
+        copy.start()
+    summed = jnp.sum(cnt_ref[...], axis=0)
+    lane = lax.broadcasted_iota(jnp.int32, summed.shape, 1)
+    for step in range(removed_ref.shape[0]):
+        removed_ref[step] = jnp.sum(jnp.where(lane == step, summed, 0)) // 2
+    for copy in copies:
+        copy.wait()
 
 
 def on_device(n, adj_diag, adj_right, alive_diag, alive_right, truss_k):
     words, t = adj_diag.shape
     vmem = pl.BlockSpec(memory_space=pltpu.VMEM)
     smem = pl.BlockSpec(memory_space=pltpu.SMEM)
-    return pl.pallas_call(
+    hbm = pl.BlockSpec(memory_space=pltpu.HBM)
+    args = [
+        pltpu.with_memory_space_constraint(v, pltpu.HBM)
+        for v in (adj_diag, adj_right, alive_diag, alive_right)
+    ]
+    support, counts = pl.pallas_call(
         functools.partial(kernel, n),
         out_shape=(
             jax.ShapeDtypeStruct((t, 2 * t), F32),
-            jax.ShapeDtypeStruct((3,), jnp.int32),
+            jax.ShapeDtypeStruct((n, 1, 128), jnp.int32),
         ),
-        in_specs=[smem] + [pl.BlockSpec(memory_space=pltpu.MemorySpace.HBM)] * 4,
-        out_specs=(vmem, smem),
+        in_specs=[hbm] * 5,
+        out_specs=(vmem, vmem),
         scratch_shapes=[
+            pltpu.SMEM((1,), jnp.int32),
             pltpu.VMEM((4, words, t), jnp.int32),
             pltpu.VMEM((2, words, t), jnp.int32),
             pltpu.VMEM((6, words, t), jnp.int32),
@@ -283,6 +310,7 @@
             pltpu.VMEM((t, t), F32),
             pltpu.VMEM((1, 128), jnp.int32),
             pltpu.VMEM((n - 1, 1, 128), jnp.int32),
+            pltpu.SemaphoreType.DMA,
             pltpu.SemaphoreType.DMA((4,)),
             pltpu.SemaphoreType.DMA((6, 2)),
             pltpu.SemaphoreType.DMA((12,)),
@@ -291,7 +319,18 @@
             pltpu.SemaphoreType.DMA,
         ],
         compiler_params=pltpu.CompilerParams(collective_id=0, has_side_effects=True, vmem_limit_bytes=24 * 2**20),
-    )(truss_k, *[pltpu.with_memory_space_constraint(v, pltpu.HBM) for v in (adj_diag, adj_right, alive_diag, alive_right)])
+    )(truss_k, *args)
+    return pl.pallas_call(
+        finish,
+        out_shape=(
+            jax.ShapeDtypeStruct((t, 2 * t), F32),
+            jax.ShapeDtypeStruct((ITERS,), jnp.int32),
+        ),
+        in_specs=[vmem, vmem],
+        out_specs=(hbm, smem),
+        scratch_shapes=[pltpu.SemaphoreType.DMA((4,))],
+        compiler_params=pltpu.CompilerParams(vmem_limit_bytes=2**20),
+    )(support, counts)
 
 
 def solution(mesh):

time: 26.4 us -> 24.6 us (0.932)
  local copies, waits for them, and re-layouts: 1.83 us -> 0 us
    pallas_call x0 -> x1, Pallas kernels: none -> 1.87 us  [on_device(): pl.pallas_call(finish, out_shape=(jax.ShapeDtypeStruct((t, 2 * t), F32),...]
    pallas_call x1, Pallas kernels: 23.1 us -> 21.2 us  [on_device(): pl.pallas_call(functools.partial(kernel, n), out_shape=(jax.ShapeDtypeStr...]
    unnamed x2 -> x0, local copies, waits for them, and re-layouts: 1.83 us -> none
where the time goes in v3:
time: 24.6 us; the launch traced here: 24.4 us
  Pallas kernels  23.1 us (94%)
  between operations  1.29 us (5%)
    pallas_call x1, Pallas kernels, on_device(): pl.pallas_call(functools.partial(kernel, n), out_shape=(jax.ShapeDtypeStr...  21.2 us
    pallas_call x1, Pallas kernels, on_device(): pl.pallas_call(finish, out_shape=(jax.ShapeDtypeStruct((t, 2 * t), F32),...  1.87 us

profile of v3, /device:TPU:0, one launch (start us, length us, event | category | flops | bytes accessed | tf_op | source)
XLA Modules:
  0.0 24.4 jit_solution(11951037025998292746)
XLA Ops:
  1.3 21.2 %shard_map.68 = (f32[512,1024]{1,0:T(8,128)S(1)}, s32[32,1,128]{2,1,0:T(1,128)S(1)}) custom-call(s32[1]{0:T(128)S(6)} %copy.7.k_ref, s32[16,512]{1,0:T(8,128)} %ad_ref.1, s32[16,512]{1,0:T(8,128)} %ar_ref.1, s32[16,512]{1,0:T(8,128)} %ld_ref.1, s32[16,512]{1,0:T(8,128)} %lr_ref.1), custom_call_target="tpu_custom_call" | custom-call | tf_op jit(solution)/shard_map/pallas_call | solution.py:291
  22.5 1.9 %shard_map.69 = (f32[512,1024]{1,0:T(8,128)}, s32[3]{0:T(128)}) custom-call(f32[512,1024]{1,0:T(8,128)S(1)} %get-tuple-element.4.support_ref, s32[32,1,128]{2,1,0:T(1,128)S(1)} %get-tuple-element.5.cnt_ref), custom_call_target="tpu_custom_call" | custom-call | tf_op jit(solution)/shard_map/pallas_call | solution.py:323

commit v4 on v3

--- a/solution.py
+++ b/solution.py
@@ -45,7 +45,8 @@
         )
         return carry
 
-    lax.fori_loop(1, n, greet, 0)
+    for d in (1, n - 1, 2, n - 2):
+        greet(d, 0)
     loads = [
         pltpu.make_async_copy(src, raw.at[i], raw_sems.at[i])
         for i, src in enumerate((ad_ref, ar_ref, ld_ref, lr_ref))
@@ -54,6 +55,7 @@
         load.start()
     k_load = pltpu.make_async_copy(k_ref, k_smem, k_sem)
     k_load.start()
+    lax.fori_loop(3, n - 2, greet, 0)
     for load in loads:
         load.wait()
     own[0] = raw[0] & raw[2]
@@ -162,6 +164,11 @@
     def between(j):
         return dot_nt(x[j, :, t:], x[j + 1, :, : 2 * t])
 
+    def between_plain(j):
+        return jnp.dot(x[j, :, A], x[j + 1, :, W], preferred_element_type=F32) + jnp.dot(
+            x[j, :, W], x[j, :, A], preferred_element_type=F32
+        )
+
     counts = []
 
     def own_count(old_w, new_w, old_a, new_a):
@@ -180,35 +187,34 @@
     arrive(1)
     put_within(halo.at[1], 0)
     _, am = keep(between(0), 0, A)
-    arrive(3)
-
-    @pl.when(jnp.logical_not(even))
-    def _():
-        for piece in to_left:
-            piece.start()
-
     arrive(0)
     for rows, _, bits in unpack(halo.at[0], False):
         spare[rows, :] = bits
     x[0, :, AT] = dot_nt(eye[...], spare[...]).astype(F8)
     _, wm = keep(inside(0), 0, W)
+    x[0, :, W] = wm.astype(F8)
+    x[0, :, A] = am.astype(F8)
+    x[1, :, W] = w0.astype(F8)
+    put_transposed(0)
+    arrive(3)
+
+    @pl.when(jnp.logical_not(even))
+    def _():
+        for piece in to_left:
+            piece.start()
+
     put_within(halo.at[3], 2)
     old_a, a0 = keep(psum_btw[...] + dot_nt(x[1, :, A], x[2, :, W]), 1, A)
     own_count(old_w, w0, old_a, a0)
     arrive(4)
     put_across(halo.at[4], 2)
-    put_transposed(2)
     _, w1 = keep(psum_next[...] + dot_nt(x[2, :, t:], x[2, :, t:]), 2, W)
     arrive(5)
     put_within(halo.at[5], 3)
-    _, a1 = keep(between(2), 2, A)
-    x[0, :, W] = wm.astype(F8)
-    x[0, :, A] = am.astype(F8)
-    x[1, :, W] = w0.astype(F8)
+    _, a1 = keep(between_plain(2), 2, A)
     x[1, :, A] = a0.astype(F8)
     x[2, :, W] = w1.astype(F8)
     x[2, :, A] = a1.astype(F8)
-    put_transposed(0)
     put_transposed(1)
 
     _, am = keep(between(0), 0, A)
@@ -221,11 +227,10 @@
     x[1, :, A] = a0.astype(F8)
     x[2, :, W] = w1.astype(F8)
     put_transposed(0)
-    put_transposed(1)
 
     support_w = inside(1)
     old_w, w0 = keep(support_w, 1, W)
-    support_a = between(1)
+    support_a = between_plain(1)
     old_a, a0 = keep(support_a, 1, A)
     own_count(old_w, w0, old_a, a0)
     lane = lax.broadcasted_iota(jnp.int32, (1, 128), 1)

time: 24.6 us -> 23.8 us (0.967)
  Pallas kernels: 23.1 us -> 22.3 us
    pallas_call x1, Pallas kernels: 21.2 us -> 20.4 us  [on_device(): pl.pallas_call(functools.partial(kernel, n), out_shape=(jax.ShapeDtypeStr...]
where the time goes in v4:
time: 23.8 us; the launch traced here: 23.6 us
  Pallas kernels  22.3 us (94%)
  between operations  1.29 us (5%)
    pallas_call x1, Pallas kernels, on_device(): pl.pallas_call(functools.partial(kernel, n), out_shape=(jax.ShapeDtypeStr...  20.4 us
    pallas_call x1, Pallas kernels, on_device(): pl.pallas_call(finish, out_shape=(jax.ShapeDtypeStruct((t, 2 * t), F32),...  1.87 us

profile of v4, /device:TPU:0, one launch (start us, length us, event | category | flops | bytes accessed | tf_op | source)
XLA Modules:
  0.0 23.6 jit_solution(10623880856207365018)
XLA Ops:
  1.3 20.4 %shard_map.68 = (f32[512,1024]{1,0:T(8,128)S(1)}, s32[32,1,128]{2,1,0:T(1,128)S(1)}) custom-call(s32[1]{0:T(128)S(6)} %copy.7.k_ref, s32[16,512]{1,0:T(8,128)} %ad_ref.1, s32[16,512]{1,0:T(8,128)} %ar_ref.1, s32[16,512]{1,0:T(8,128)} %ld_ref.1, s32[16,512]{1,0:T(8,128)} %lr_ref.1), custom_call_target="tpu_custom_call" | custom-call | tf_op jit(solution)/shard_map/pallas_call | solution.py:296
  21.7 1.9 %shard_map.69 = (f32[512,1024]{1,0:T(8,128)}, s32[3]{0:T(128)}) custom-call(f32[512,1024]{1,0:T(8,128)S(1)} %get-tuple-element.4.support_ref, s32[32,1,128]{2,1,0:T(1,128)S(1)} %get-tuple-element.5.cnt_ref), custom_call_target="tpu_custom_call" | custom-call | tf_op jit(solution)/shard_map/pallas_call | solution.py:328
